TPU v7x, 32 devices: a whole 2x2x4 slice. The times are simulated.
32 devices in a mesh: section: 2 (over y), pen: 8 (over z, x), slab: 2 (over core).
Axes of the slice: x: 2, y: 2, z: 4, core: 2. Of those that a mesh axis runs over, the one named last changes fastest.
Arguments:
- velocity: float32 [3, 48, 48, 48], P(None, ('section', 'pen'), 'slab'), may hold values from -6 to 6
- vorticity: float32 [3, 48, 48, 48], P(None, ('section', 'pen'), 'slab'), may hold values from -6 to 6
- velocity_modes: float32 [3, 32, 32, 2, 32], P(None, None, ('section', 'pen'), None, 'slab'), may hold values from -6 to 6
Outputs:
- rhs_modes: float32 [3, 32, 32, 2, 32], P(None, None, ('section', 'pen'), None, 'slab')
All inputs are finite; a program needn't handle non-finite values.
Results may differ from a plain program's by a relative error of at most 0.000057.
Values sent between devices are 32-bit elements; how exact they have to be, the bound alone decides.
A program may use at most 64 MiB of HBM per device.

v0:
```python
import math
import jax
import jax.numpy as jnp
from jax import lax
from jax.sharding import PartitionSpec as P

highest = lax.Precision.HIGHEST


def signed_modes(index, count):
    return jnp.where(index < count // 2, index, index - count)


def discrete_fourier_tables(length, keep_count):
    modes = signed_modes(jnp.arange(keep_count, dtype=jnp.int32), keep_count)
    mode_positions = jnp.arange(length, dtype=jnp.int32)
    phase = jnp.remainder(modes[:, None] * mode_positions[None, :], length).astype(jnp.float32)
    angles = 2.0 * math.pi / length * phase
    factor = 1.0 / math.sqrt(length)
    return (jnp.cos(angles) * factor, jnp.sin(angles) * factor)


def complex_apply(form, cosine, sine, real_part, imag_part):
    out_real = jnp.einsum(form, cosine, real_part, precision=highest) + jnp.einsum(
        form, sine, imag_part, precision=highest
    )
    out_imag = jnp.einsum(form, cosine, imag_part, precision=highest) - jnp.einsum(
        form, sine, real_part, precision=highest
    )
    return (out_real, out_imag)


def per_device(velocity, vorticity, velocity_modes):
    grid_cells = velocity.shape[3]
    keep_count = velocity_modes.shape[1]
    cross_product = jnp.stack(
        [
            velocity[1] * vorticity[2] - velocity[2] * vorticity[1],
            velocity[2] * vorticity[0] - velocity[0] * vorticity[2],
            velocity[0] * vorticity[1] - velocity[1] * vorticity[0],
        ]
    )
    slabs = lax.axis_size("slab")
    block_modes = keep_count // slabs
    cosine_table, sine_table = discrete_fourier_tables(grid_cells, keep_count)
    cols_real = cosine_table.T.reshape(grid_cells, slabs, block_modes)
    cols_imag = (-sine_table).T.reshape(grid_cells, slabs, block_modes)
    column_table = jnp.stack([cols_real, cols_imag], axis=2).reshape(grid_cells, 2 * keep_count)
    first_pass = jnp.einsum("czyx,xj->czyj", cross_product, column_table, precision=highest)
    block = lax.all_to_all(first_pass, "slab", split_axis=3, concat_axis=2, tiled=True)
    out_real, out_imag = complex_apply(
        "ky,czyj->czkj",
        cosine_table,
        sine_table,
        block[..., :block_modes],
        block[..., block_modes:],
    )
    second_pass = jnp.concatenate([out_real, out_imag], axis=-1)
    halves = lax.axis_size("section")
    pens = lax.axis_size("pen")
    rows_ky = keep_count // (halves * pens)
    block = lax.all_to_all(second_pass, ("section", "pen"), split_axis=2, concat_axis=1, tiled=True)
    out_real, out_imag = complex_apply(
        "kz,czyj->ckyj",
        cosine_table,
        sine_table,
        block[..., :block_modes],
        block[..., block_modes:],
    )
    third_pass = jnp.concatenate([out_real, out_imag], axis=-1)
    group_index = lax.axis_index("section") * pens + lax.axis_index("pen")
    modes_z = signed_modes(jnp.arange(keep_count, dtype=jnp.int32), keep_count)[:, None, None]
    modes_y = signed_modes(
        group_index * rows_ky + jnp.arange(rows_ky, dtype=jnp.int32), keep_count
    )[None, :, None]
    modes_x = signed_modes(
        lax.axis_index("slab") * block_modes + jnp.arange(block_modes, dtype=jnp.int32), keep_count
    )[None, None, :]
    limit = -(keep_count // 2)
    keep_mask = ((modes_x != limit) & (modes_y != limit) & (modes_z != limit)).astype(jnp.float32)
    waves = (modes_x.astype(jnp.float32), modes_y.astype(jnp.float32), modes_z.astype(jnp.float32))
    ksq = waves[0] * waves[0] + waves[1] * waves[1] + waves[2] * waves[2]
    denom = jnp.maximum(ksq, 1.0)
    parts = []
    for which in range(2):
        chosen = third_pass[..., which * block_modes : (which + 1) * block_modes]
        comp = [chosen[c] for c in range(3)]
        inner = (waves[0] * comp[0] + waves[1] * comp[1] + waves[2] * comp[2]) / denom
        parts.append(jnp.stack([comp[c] - waves[c] * inner for c in range(3)]))
    projected = jnp.stack(parts, axis=3)
    visc = 0.5 / (keep_count // 2) ** 2
    return (
        projected * keep_mask[None, :, :, None, :]
        - visc * ksq[None, :, :, None, :] * velocity_modes
    )


def solution(mesh):
    return jax.shard_map(
        per_device,
        mesh=mesh,
        in_specs=(
            P(None, ("section", "pen"), "slab", None),
            P(None, ("section", "pen"), "slab", None),
            P(None, None, ("section", "pen"), None, "slab"),
        ),
        out_specs=P(None, None, ("section", "pen"), None, "slab"),
        check_vma=False,
    )
```

profile of v0, /device:TPU:0, one launch (start us, length us, event | category | flops | bytes accessed | tf_op | source)
XLA Modules:
  0.0 32.4 jit_solution(18080253306396795170)
XLA Ops:
  0.0 0.2 cosine_multiply_fusion.1
  0.2 0.9 %multiply_subtract_fusion.2 = (f32[1,3,24,48]{3,2,1,0:T(8,128)S(1)}, f32[1,3,24,48]{3,2,1,0:T(8,128)S(1)}, f32[1,3,24,48]{3,2,1,0:T(8,128)S(1)}) fusion(f32[3,3,24,48]{3,2,1,0:T(8,128)} %param.4, f32[3,3,24,48]{3,2,1,0:T(8,128)} %param.3), kind=kLoop, calls=%fused_computation.28 | loop fusion | flops 31104 | bytes 124416 | tf_op jit(solution)/shard_map/sub | solution.py:38
  1.1 0.3 %fusion.10 = f32[3,3,24,64]{3,2,1,0:T(8,128)S(1)} fusion(f32[48,64,1,1]{0,1,3,2:T(8,128)S(1)} %bitcast.64, f32[1,3,24,48]{3,2,1,0:T(8,128)S(1)} %get-tuple-element.10, f32[1,3,24,48]{3,2,1,0:T(8,128)S(1)} %get-tuple-element.11, f32[1,3,24,48]{3,2,1,0:T(8,128)S(1)} %get-tuple-element.9), kind=kOutput, calls=%fused_computation.15 | convolution fusion | flops 7983360 | bytes 109056 | tf_op jit(solution)/shard_map/czyx,xj->czyj/dot_general | solution.py:49
  1.4 0.2 copy.19
  1.6 0.9 %reshape.210 = f32[2,1,6912]{2,1,0:T(1,128)} reshape(f32[64,3,3,24]{3,2,1,0:T(4,128)S(1)} %bitcast.59) | data formatting | bytes 110592
  2.6 3.3 %all-to-all-start = ((f32[2,1,6912]{2,1,0:T(1,128)}), f32[2,1,6912]{2,1,0:T(1,128)S(1)}, u32[]{:S(2)}, u32[]{:S(2)}) async-start(f32[2,1,6912]{2,1,0:T(1,128)} %reshape.210), calls=%async_computation | async-start | bytes 110592 | tf_op jit(solution)/shard_map/all_to_all | solution.py:50
  5.9 1.4 %all-to-all-done = f32[2,1,6912]{2,1,0:T(1,128)S(1)} async-done(((f32[2,1,6912]{2,1,0:T(1,128)}), f32[2,1,6912]{2,1,0:T(1,128)S(1)}, u32[]{:S(2)}, u32[]{:S(2)}) %all-to-all-start) | async-done | bytes 55328 | tf_op jit(solution)/shard_map/all_to_all | solution.py:50
  7.2 0.5 %broadcast.464 = f32[]{:T(128)} broadcast(f32[]{:T(128)} %constant.195), dimensions={} | broadcast | bytes 8 | tf_op jit(solution)/shard_map/all_to_all | solution.py:50
  7.7 0.7 %reduce = f32[2,6912]{1,0:T(2,128)S(1)} reduce(f32[2,1,6912]{2,1,0:T(1,128)S(1)} %all-to-all-done, f32[]{:T(128)} %broadcast.464), dimensions={1}, to_apply=%all_to_all.26.reduce_sub_computation | reduce | bytes 110596 | tf_op jit(solution)/shard_map/all_to_all | solution.py:50
  8.5 0.3 reshape.211
  8.8 0.2 copy.20
  8.9 0.5 %fusion.7 = f32[3,3,16,32]{3,2,1,0:T(8,128)S(1)} fusion(f32[3,3,48,32]{3,2,1,0:T(8,128)S(1)} %bitcast.54, s32[32]{0:T(128)S(1)} %compare_select_fusion.3), kind=kOutput, calls=%fused_computation.11 | convolution fusion | flops 2669568 | bytes 73856 | tf_op jit(solution)/shard_map/ky,czyj->czkj/dot_general | solution.py:24
  9.5 0.6 %fusion.5 = f32[3,3,16,32]{3,2,1,0:T(8,128)S(1)} fusion(f32[3,3,48,32]{3,2,1,0:T(8,128)S(1)} %bitcast.55, s32[32]{0:T(128)S(1)} %compare_select_fusion.3), kind=kOutput, calls=%fused_computation.9 | convolution fusion | flops 2669568 | bytes 73856 | tf_op jit(solution)/shard_map/ky,czyj->czkj/dot_general | solution.py:27
  10.1 0.6 %fusion.1 = f32[3,3,32,16]{2,3,1,0:T(8,128)S(1)} fusion(f32[3,3,16,32]{3,2,1,0:T(8,128)S(1)} %fusion.7, f32[3,3,48,32]{3,2,1,0:T(8,128)S(1)} %bitcast.56, s32[32]{0:T(128)S(1)} %compare_select_fusion.3), kind=kOutput, calls=%fused_computation.3 | convolution fusion | flops 2674176 | bytes 92288 | tf_op jit(solution)/shard_map/ky,czyj->czkj/dot_general | solution.py:24
  10.7 0.5 %fusion = f32[3,3,32,16]{2,3,1,0:T(8,128)S(1)} fusion(f32[3,3,16,32]{3,2,1,0:T(8,128)S(1)} %fusion.5, f32[3,3,48,32]{3,2,1,0:T(8,128)S(1)} %bitcast.57, s32[32]{0:T(128)S(1)} %compare_select_fusion.3), kind=kOutput, calls=%fused_computation.1 | convolution fusion | flops 2674176 | bytes 92288 | tf_op jit(solution)/shard_map/ky,czyj->czkj/dot_general | solution.py:27
  11.3 0.1 copy.23
  11.4 0.8 %reshape.212 = f32[16,1,576]{2,1,0:T(1,128)} reshape(f32[32,3,3,32]{3,2,1,0:T(4,128)S(1)} %bitcast.61) | data formatting | bytes 73728
  12.2 8.3 %all-to-all-start.1 = ((f32[16,1,576]{2,1,0:T(1,128)}), f32[16,1,576]{2,1,0:T(1,128)S(1)}, u32[]{:S(2)}, u32[]{:S(2)}) async-start(f32[16,1,576]{2,1,0:T(1,128)} %reshape.212), calls=%async_computation.1 | async-start | bytes 81920 | tf_op jit(solution)/shard_map/all_to_all | solution.py:62
  20.7 0.1 broadcast_add_fusion
  20.7 0.1 add_multiply_fusion
  20.8 0.1 broadcast_and_fusion
  20.9 0.1 and_convert_fusion
  21.0 7.0 %all-to-all-done.1 = f32[16,1,576]{2,1,0:T(1,128)S(1)} async-done(((f32[16,1,576]{2,1,0:T(1,128)}), f32[16,1,576]{2,1,0:T(1,128)S(1)}, u32[]{:S(2)}, u32[]{:S(2)}) %all-to-all-start.1) | async-done | bytes 36896 | tf_op jit(solution)/shard_map/all_to_all | solution.py:62
  28.0 0.7 %reduce.1 = f32[16,576]{1,0:T(8,128)S(1)} reduce(f32[16,1,576]{2,1,0:T(1,128)S(1)} %all-to-all-done.1, f32[]{:T(128)} %broadcast.464), dimensions={1}, to_apply=%all_to_all.30.reduce_sub_computation | reduce | bytes 73732 | tf_op jit(solution)/shard_map/all_to_all | solution.py:62
  28.6 0.1 reshape.213
  28.8 0.1 copy.25
  28.9 0.2 fusion.118
  29.1 0.1 copy.37
  29.2 0.3 %fusion.25 = f32[3,2,16,32]{3,2,1,0:T(8,128)S(1)} fusion(f32[3,48,2,16]{1,3,2,0:T(8,128)S(1)} %copy.37, s32[32]{0:T(128)S(1)} %compare_select_fusion.3), kind=kOutput, calls=%fused_computation.40 | convolution fusion | flops 1784832 | bytes 30848 | tf_op jit(solution)/shard_map/kz,czyj->ckyj/dot_general | solution.py:27
  29.5 0.1 copy.36
  29.6 0.3 %fusion.27 = f32[3,2,16,32]{3,2,1,0:T(8,128)S(1)} fusion(f32[3,48,2,16]{1,3,2,0:T(8,128)S(1)} %copy.36, s32[32]{0:T(128)S(1)} %compare_select_fusion.3), kind=kOutput, calls=%fused_computation.42 | convolution fusion | flops 1784832 | bytes 30848 | tf_op jit(solution)/shard_map/kz,czyj->ckyj/dot_general | solution.py:24
  30.0 0.3 %fusion.2 = f32[3,32,2,16]{1,3,2,0:T(8,128)S(1)} fusion(f32[3,2,16,32]{3,2,1,0:T(8,128)S(1)} %fusion.25, f32[3,48,2,16]{1,3,2,0:T(8,128)S(1)} %copy.36, s32[32]{0:T(128)S(1)} %compare_select_fusion.3), kind=kOutput, calls=%fused_computation.5 | convolution fusion | flops 1787904 | bytes 43136 | tf_op jit(solution)/shard_map/kz,czyj->ckyj/dot_general | solution.py:27
  30.3 0.3 %fusion.3 = f32[3,32,2,16]{1,3,2,0:T(8,128)S(1)} fusion(f32[3,2,16,32]{3,2,1,0:T(8,128)S(1)} %fusion.27, f32[3,48,2,16]{1,3,2,0:T(8,128)S(1)} %copy.37, s32[32]{0:T(128)S(1)} %compare_select_fusion.3), kind=kOutput, calls=%fused_computation.7 | convolution fusion | flops 1787904 | bytes 43136 | tf_op jit(solution)/shard_map/kz,czyj->ckyj/dot_general | solution.py:24
  30.6 0.1 multiply_subtract_fusion.8
  30.7 0.1 multiply_subtract_fusion.4
  30.8 0.0 copy-start
  30.8 0.9 %copy-done = f32[3,32,2,2,16]{1,4,3,2,0:T(8,128)S(1)} copy-done((f32[3,32,2,2,16]{1,4,3,2,0:T(8,128)S(1)}, f32[3,32,2,2,16]{1,4,3,2,0:T(8,128)}, u32[]{:S(2)}) %copy-start) | copy-done | bytes 24600
  31.7 0.6 %copy.29 = f32[3,32,2,2,16]{1,4,3,2,0:T(8,128)} copy(f32[3,32,2,2,16]{1,4,2,0,3:T(8,128)S(1)} %fusion.16) | data formatting | bytes 49152 | tf_op jit(solution)/shard_map/sub | solution.py:93
  (16 shorter events, 0.1 us)
Async XLA Ops:
  2.6 4.7 %all-to-all-start = ((f32[2,1,6912]{2,1,0:T(1,128)}), f32[2,1,6912]{2,1,0:T(1,128)S(1)}, u32[]{:S(2)}, u32[]{:S(2)}) async-start(f32[2,1,6912]{2,1,0:T(1,128)} %reshape.210), calls=%async_computation | async-start | bytes 110592 | tf_op jit(solution)/shard_map/all_to_all | solution.py:50
  12.2 15.8 %all-to-all-start.1 = ((f32[16,1,576]{2,1,0:T(1,128)}), f32[16,1,576]{2,1,0:T(1,128)S(1)}, u32[]{:S(2)}, u32[]{:S(2)}) async-start(f32[16,1,576]{2,1,0:T(1,128)} %reshape.212), calls=%async_computation.1 | async-start | bytes 81920 | tf_op jit(solution)/shard_map/all_to_all | solution.py:62
  30.8 0.9 %copy-start = (f32[3,32,2,2,16]{1,4,3,2,0:T(8,128)S(1)}, f32[3,32,2,2,16]{1,4,3,2,0:T(8,128)}, u32[]{:S(2)}) copy-start(f32[3,32,2,2,16]{1,4,3,2,0:T(8,128)} %param.5) | copy-start | bytes 73732
where the time goes:
time: 32.7 us; the launch traced here: 32.4 us
  starting transfers between devices  11.6 us (35%)
  waiting for transfers between devices  8.39 us (26%)
  local copies, waits for them, and re-layouts  5.12 us (16%)
  matrix products  4 us (12%)
  other arithmetic  3 us (9%)
    all_to_all x1, starting transfers between devices, per_device(): lax.all_to_all(second_pass, ('section', 'pen'), split_axis=2, concat_axis...  8.34 us
    all_to_all x1, waiting for transfers between devices, per_device(): lax.all_to_all(second_pass, ('section', 'pen'), split_axis=2, concat_axis...  7.01 us
    all_to_all x1, starting transfers between devices, per_device(): lax.all_to_all(first_pass, 'slab', split_axis=3, concat_axis=2, tiled=True)  3.28 us
    unnamed x8, local copies, waits for them, and re-layouts  3.2 us
    all_to_all x1, waiting for transfers between devices, per_device(): lax.all_to_all(first_pass, 'slab', split_axis=3, concat_axis=2, tiled=True)  1.38 us
    dot_general x2, matrix products, complex_apply(): jnp.einsum(form, cosine, imag_part, precision=highest)  0.96 us
    dot_general x2, matrix products, complex_apply(): jnp.einsum(form, sine, imag_part, precision=highest)  0.95 us
    dot_general x2, matrix products, complex_apply(): jnp.einsum(form, cosine, real_part, precision=highest)  0.89 us
  transfers between devices with their start and end apart: 2, of which 2 were waited for; matrix products, arithmetic and copies ran while one was open for 1% of the time, Pallas kernels for 0%

commit v1 on v0

--- a/solution.py
+++ b/solution.py
@@ -31,6 +31,15 @@
 
 
 def per_device(velocity, vorticity, velocity_modes):
+
+    def load_leaves(content, which_axis):
+        extra = lax.axis_size(which_axis)
+        f_now = jnp.split(content, extra, axis=2)
+        left_arr = jnp.stack(f_now)
+        y2 = lax.all_to_all(left_arr, which_axis, 0, 0)
+        n_now = jnp.concatenate(y2, axis=1)
+        return n_now
+
     grid_cells = velocity.shape[3]
     keep_count = velocity_modes.shape[1]
     cross_product = jnp.stack(
@@ -59,7 +68,7 @@
     halves = lax.axis_size("section")
     pens = lax.axis_size("pen")
     rows_ky = keep_count // (halves * pens)
-    block = lax.all_to_all(second_pass, ("section", "pen"), split_axis=2, concat_axis=1, tiled=True)
+    block = load_leaves(second_pass, ("section", "pen"))
     out_real, out_imag = complex_apply(
         "kz,czyj->ckyj",
         cosine_table,

time: 32.7 us -> 34.3 us (1.049)
  other arithmetic: 3 us -> 4.51 us
    unnamed x0 -> x15, other arithmetic: none -> 1.42 us
    another operation x0 -> x1, local copies, waits for them, and re-layouts: none -> 0.94 us  [load_leaves(): left_arr = jnp.stack(f_now)]
    unnamed x8, local copies, waits for them, and re-layouts: 3.2 us -> 2.35 us
where the time goes in v1:
time: 34.3 us; the launch traced here: 33.9 us
  starting transfers between devices  11.6 us (34%)
  waiting for transfers between devices  8.39 us (24%)
  local copies, waits for them, and re-layouts  5.05 us (15%)
  other arithmetic  4.51 us (13%)
  matrix products  4.01 us (12%)
    all_to_all x1, starting transfers between devices, load_leaves(): y2 = lax.all_to_all(left_arr, which_axis, 0, 0)  8.34 us
    all_to_all x1, waiting for transfers between devices, load_leaves(): y2 = lax.all_to_all(left_arr, which_axis, 0, 0)  7.01 us
    all_to_all x1, starting transfers between devices, per_device(): lax.all_to_all(first_pass, 'slab', split_axis=3, concat_axis=2, tiled=True)  3.28 us
    unnamed x8, local copies, waits for them, and re-layouts  2.35 us
    unnamed x15, other arithmetic  1.42 us
    all_to_all x1, waiting for transfers between devices, per_device(): lax.all_to_all(first_pass, 'slab', split_axis=3, concat_axis=2, tiled=True)  1.38 us
    dot_general x2, matrix products, complex_apply(): jnp.einsum(form, cosine, imag_part, precision=highest)  0.96 us
    dot_general x2, matrix products, complex_apply(): jnp.einsum(form, sine, imag_part, precision=highest)  0.94 us
  transfers between devices with their start and end apart: 2, of which 2 were waited for; matrix products, arithmetic and copies ran while one was open for 1% of the time, Pallas kernels for 0%

profile of v1, /device:TPU:0, one launch (start us, length us, event | category | flops | bytes accessed | tf_op | source)
XLA Modules:
  0.0 33.9 jit_solution(9870490536624011459)
XLA Ops:
  0.0 0.2 cosine_multiply_fusion.1
  0.2 0.9 %multiply_subtract_fusion.2 = (f32[1,3,24,48]{3,2,1,0:T(8,128)S(1)}, f32[1,3,24,48]{3,2,1,0:T(8,128)S(1)}, f32[1,3,24,48]{3,2,1,0:T(8,128)S(1)}) fusion(f32[3,3,24,48]{3,2,1,0:T(8,128)} %param.4, f32[3,3,24,48]{3,2,1,0:T(8,128)} %param.3), kind=kLoop, calls=%fused_computation.105 | loop fusion | flops 31104 | bytes 124416 | tf_op jit(solution)/shard_map/sub | solution.py:47
  1.1 0.3 fusion.57
  1.4 0.2 copy.44
  1.6 0.9 %reshape.218 = f32[2,1,6912]{2,1,0:T(1,128)} reshape(f32[64,3,3,24]{3,2,1,0:T(4,128)S(1)} %bitcast.119) | data formatting | bytes 110592
  2.6 3.3 %all-to-all-start = ((f32[2,1,6912]{2,1,0:T(1,128)}), f32[2,1,6912]{2,1,0:T(1,128)S(1)}, u32[]{:S(2)}, u32[]{:S(2)}) async-start(f32[2,1,6912]{2,1,0:T(1,128)} %reshape.218), calls=%async_computation | async-start | bytes 110592 | tf_op jit(solution)/shard_map/all_to_all | solution.py:59
  5.9 1.4 %all-to-all-done = f32[2,1,6912]{2,1,0:T(1,128)S(1)} async-done(((f32[2,1,6912]{2,1,0:T(1,128)}), f32[2,1,6912]{2,1,0:T(1,128)S(1)}, u32[]{:S(2)}, u32[]{:S(2)}) %all-to-all-start) | async-done | bytes 55328 | tf_op jit(solution)/shard_map/all_to_all | solution.py:59
  7.2 0.5 %broadcast.464 = f32[]{:T(128)} broadcast(f32[]{:T(128)} %constant.319), dimensions={} | broadcast | bytes 8 | tf_op jit(solution)/shard_map/all_to_all | solution.py:59
  7.7 0.7 %reduce = f32[2,6912]{1,0:T(2,128)S(1)} reduce(f32[2,1,6912]{2,1,0:T(1,128)S(1)} %all-to-all-done, f32[]{:T(128)} %broadcast.464), dimensions={1}, to_apply=%all_to_all.16.reduce_sub_computation | reduce | bytes 110596 | tf_op jit(solution)/shard_map/all_to_all | solution.py:59
  8.5 0.3 reshape.219
  8.8 0.2 copy.45
  8.9 0.6 %fusion.5 = f32[3,3,16,32]{3,2,1,0:T(8,128)S(1)} fusion(f32[3,3,48,32]{3,2,1,0:T(8,128)S(1)} %bitcast.114, s32[32]{0:T(128)S(1)} %compare_select_fusion.3), kind=kOutput, calls=%fused_computation.39 | convolution fusion | flops 2669568 | bytes 73856 | tf_op jit(solution)/shard_map/ky,czyj->czkj/dot_general | solution.py:27
  9.5 0.5 %fusion.7 = f32[3,3,16,32]{3,2,1,0:T(8,128)S(1)} fusion(f32[3,3,48,32]{3,2,1,0:T(8,128)S(1)} %bitcast.115, s32[32]{0:T(128)S(1)} %compare_select_fusion.3), kind=kOutput, calls=%fused_computation.41 | convolution fusion | flops 2669568 | bytes 73856 | tf_op jit(solution)/shard_map/ky,czyj->czkj/dot_general | solution.py:24
  10.1 0.5 %fusion = f32[3,3,32,16]{2,3,1,0:T(8,128)S(1)} fusion(f32[3,3,16,32]{3,2,1,0:T(8,128)S(1)} %fusion.5, f32[3,3,48,32]{3,2,1,0:T(8,128)S(1)} %bitcast.116, s32[32]{0:T(128)S(1)} %compare_select_fusion.3), kind=kOutput, calls=%fused_computation.1 | convolution fusion | flops 2674176 | bytes 92288 | tf_op jit(solution)/shard_map/ky,czyj->czkj/dot_general | solution.py:27
  10.6 0.6 %fusion.1 = f32[3,3,32,16]{2,3,1,0:T(8,128)S(1)} fusion(f32[3,3,16,32]{3,2,1,0:T(8,128)S(1)} %fusion.7, f32[3,3,48,32]{3,2,1,0:T(8,128)S(1)} %bitcast.117, s32[32]{0:T(128)S(1)} %compare_select_fusion.3), kind=kOutput, calls=%fused_computation.3 | convolution fusion | flops 2674176 | bytes 92288 | tf_op jit(solution)/shard_map/ky,czyj->czkj/dot_general | solution.py:24
  11.3 0.1 fusion.18
  11.4 0.1 fusion.21
  11.5 0.1 fusion.24
  11.6 0.1 fusion.27
  11.7 0.1 fusion.30
  11.8 0.1 fusion.33
  11.9 0.1 fusion.36
  12.0 0.1 fusion.39
  12.1 0.1 fusion.42
  12.2 0.1 fusion.45
  12.3 0.1 fusion.48
  12.4 0.1 fusion.51
  12.6 0.1 fusion.54
  12.7 0.1 fusion.12
  12.8 0.1 fusion.56
  12.9 0.0 copy-start
  12.9 0.9 %copy.48 = f32[16,3,3,2,32]{4,3,2,1,0:T(2,128)S(1)} copy(f32[16,3,3,2,32]{3,4,2,1,0:T(8,128)S(1)} %fusion.56) | data formatting | bytes 73728 | tf_op jit(solution)/shard_map/stack | solution.py:38
  13.8 0.8 %reshape.220 = f32[16,1,576]{2,1,0:T(1,128)} reshape(f32[16,3,3,2,32]{4,3,2,1,0:T(2,128)S(1)} %copy.48) | data formatting | bytes 73728
  14.6 8.3 %all-to-all-start.1 = ((f32[16,1,576]{2,1,0:T(1,128)}), f32[16,1,576]{2,1,0:T(1,128)S(1)}, u32[]{:S(2)}, u32[]{:S(2)}) async-start(f32[16,1,576]{2,1,0:T(1,128)} %reshape.220), calls=%async_computation.1 | async-start | bytes 81920 | tf_op jit(solution)/shard_map/all_to_all | solution.py:39
  23.1 0.1 broadcast_add_fusion
  23.2 0.1 add_multiply_fusion
  23.3 0.1 broadcast_and_fusion
  23.3 0.1 and_convert_fusion
  23.4 7.0 %all-to-all-done.1 = f32[16,1,576]{2,1,0:T(1,128)S(1)} async-done(((f32[16,1,576]{2,1,0:T(1,128)}), f32[16,1,576]{2,1,0:T(1,128)S(1)}, u32[]{:S(2)}, u32[]{:S(2)}) %all-to-all-start.1) | async-done | bytes 36896 | tf_op jit(solution)/shard_map/all_to_all | solution.py:39
  30.4 0.7 %reduce.1 = f32[16,576]{1,0:T(8,128)S(1)} reduce(f32[16,1,576]{2,1,0:T(1,128)S(1)} %all-to-all-done.1, f32[]{:T(128)} %broadcast.464), dimensions={1}, to_apply=%all_to_all.20.reduce_sub_computation | reduce | bytes 73732 | tf_op jit(solution)/shard_map/all_to_all | solution.py:39
  31.1 0.1 reshape.221
  31.3 0.2 fusion.165
  31.5 0.1 copy.61
  31.6 0.3 %fusion.72 = f32[3,2,16,32]{3,2,1,0:T(8,128)S(1)} fusion(f32[3,48,2,16]{1,3,2,0:T(8,128)S(1)} %copy.61, s32[32]{0:T(128)S(1)} %compare_select_fusion.3), kind=kOutput, calls=%fused_computation.117 | convolution fusion | flops 1784832 | bytes 30848 | tf_op jit(solution)/shard_map/kz,czyj->ckyj/dot_general | solution.py:27
  31.9 0.1 copy.60
  32.0 0.3 %fusion.74 = f32[3,2,16,32]{3,2,1,0:T(8,128)S(1)} fusion(f32[3,48,2,16]{1,3,2,0:T(8,128)S(1)} %copy.60, s32[32]{0:T(128)S(1)} %compare_select_fusion.3), kind=kOutput, calls=%fused_computation.119 | convolution fusion | flops 1784832 | bytes 30848 | tf_op jit(solution)/shard_map/kz,czyj->ckyj/dot_general | solution.py:24
  32.4 0.3 fusion.2
  32.7 0.3 fusion.3
  33.0 0.1 multiply_subtract_fusion.8
  33.1 0.1 multiply_subtract_fusion.4
  33.2 0.0 copy-done
  33.3 0.6 %copy.53 = f32[3,32,2,2,16]{1,4,3,2,0:T(8,128)} copy(f32[3,32,2,2,16]{1,4,2,0,3:T(8,128)S(1)} %fusion.63) | data formatting | bytes 49152 | tf_op jit(solution)/shard_map/sub | solution.py:102
  (16 shorter events, 0.2 us)
Async XLA Ops:
  2.6 4.7 %all-to-all-start = ((f32[2,1,6912]{2,1,0:T(1,128)}), f32[2,1,6912]{2,1,0:T(1,128)S(1)}, u32[]{:S(2)}, u32[]{:S(2)}) async-start(f32[2,1,6912]{2,1,0:T(1,128)} %reshape.218), calls=%async_computation | async-start | bytes 110592 | tf_op jit(solution)/shard_map/all_to_all | solution.py:59
  12.9 20.3 %copy-start = (f32[3,32,2,2,16]{1,4,3,2,0:T(8,128)S(1)}, f32[3,32,2,2,16]{1,4,3,2,0:T(8,128)}, u32[]{:S(2)}) copy-start(f32[3,32,2,2,16]{1,4,3,2,0:T(8,128)} %param.5) | copy-start | bytes 73732
  14.6 15.8 %all-to-all-start.1 = ((f32[16,1,576]{2,1,0:T(1,128)}), f32[16,1,576]{2,1,0:T(1,128)S(1)}, u32[]{:S(2)}, u32[]{:S(2)}) async-start(f32[16,1,576]{2,1,0:T(1,128)} %reshape.220), calls=%async_computation.1 | async-start | bytes 81920 | tf_op jit(solution)/shard_map/all_to_all | solution.py:39
